TPU v7x, 32 devices: a whole 2x2x4 slice. The times are simulated.
32 devices in a mesh: cells: 16 (over z, y, x), faces: 2 (over core).
Axes of the slice: x: 2, y: 2, z: 4, core: 2. Of those that a mesh axis runs over, the one named last changes fastest.
Arguments:
- flow_state: float32 [4, 131072], P(None, 'cells'), may hold values from -6 to 6
- source_term: float32 [4, 131072], P(None, 'cells'), may hold values from -24 to 24
- volume_rate: float32 [131072], P('cells'), may hold values from 0.5 to 4
- face_normal: float32 [3, 393216], P(None, ('cells', 'faces')), may hold values from -3 to 3
- face_owner: int32 [393216], P(('cells', 'faces')), may hold values from 0 to 8191, as said below
- face_neighbour: int32 [393216], P(('cells', 'faces')), may hold values from 0 to 9727, as said below
- face_count: int32 [32], P(('cells', 'faces')), may hold values from 1536 to 12288, as said below
- send_list: int32 [96, 256], P('cells'), may hold values from 0 to 8191
- halo_count: int32 [96], P('cells'), may hold values from 64 to 256, as said below
Outputs:
- solution_field: float32 [4, 131072], P(None, 'cells')
- residual: float32 [4, 131072], P(None, 'cells')
Inputs may be any that keep to these rules, and one draw needn't show every extreme that they name: `face_owner`: A local cell of the slot's partition; with s = g mod 12288 and t = s // 192, it lies in 128 * t to 128 * t + 127. `face_neighbour`: with s and t as for face_owner: below 8192 a local cell (128 * t + d) mod 8192 with d in 0 to 255; otherwise 8192 plus a halo slot of the slot's partition in (t mod (6)) * 256 to that plus 256 - 1. Live slots of a block are its first face_count slots; in every draw some block has all 12288 slots live. `send_list`: entries at or past the list's count are unused. `halo_count`: every partition has one list with exactly 256 entries.
All inputs are finite; a program needn't handle non-finite values.
Results may differ from a plain program's by a relative error of at most 0.0003.
Values sent between devices are 32-bit elements; how exact they have to be, the bound alone decides.
A program may use at most 64 MiB of HBM per device.

v0:
```python
import jax
import jax.numpy as jnp
import numpy as np
from jax import lax
from jax.sharding import PartitionSpec as P

ITERS = 2


def passed_along(block, axis, distance):
    devices = range(lax.axis_size(axis))
    route = [((i - distance) % len(devices), i) for i in devices]
    return lax.ppermute(block, axis, route)


def offsets(count):
    return [which + 1 for which in range(count)] + [-(which + 1) for which in range(count)]


def body(
    flow_state,
    source_term,
    volume_rate,
    face_normal,
    face_owner,
    face_neighbour,
    face_count,
    send_list,
    halo_count,
):
    highest = lax.Precision.HIGHEST
    cells_here = flow_state.shape[1]
    list_total, slot_width = send_list.shape
    shift_list = offsets(list_total // 2)
    slot_ids = lax.broadcasted_iota(jnp.int32, (list_total, slot_width), 1)
    keep_mask = (slot_ids < halo_count[:, None]).astype(jnp.float32)
    tiles = cells_here // 128
    slot_total = face_owner.shape[0]
    per_tile = slot_total // tiles
    halo_total = list_total * slot_width
    window = max(slot_width, halo_total // tiles)
    window_count = halo_total // window
    window_pick = np.arange(tiles) % window_count
    tile_ids = lax.broadcasted_iota(jnp.int32, (tiles, per_tile), 0)
    owner_tiled = face_owner.reshape(tiles, per_tile)
    neighbour_tiled = face_neighbour.reshape(tiles, per_tile)
    is_local_tiled = neighbour_tiled < cells_here
    owner_column = owner_tiled - tile_ids * 128
    local_column = jnp.where(is_local_tiled, (neighbour_tiled - tile_ids * 128) % cells_here, -1)
    halo_column = jnp.where(
        is_local_tiled, -1, neighbour_tiled - cells_here - tile_ids % window_count * window
    )
    owner_hot = (
        owner_column[:, :, None] == lax.broadcasted_iota(jnp.int32, (1, 1, 128), 2)
    ).astype(jnp.float32)
    local_hot = (
        local_column[:, :, None] == lax.broadcasted_iota(jnp.int32, (1, 1, 256), 2)
    ).astype(jnp.float32)
    halo_hot = (
        halo_column[:, :, None] == lax.broadcasted_iota(jnp.int32, (1, 1, window), 2)
    ).astype(jnp.float32)
    is_live = (
        lax.broadcasted_iota(jnp.int32, (tiles, per_tile), 0) * per_tile
        + lax.broadcasted_iota(jnp.int32, (tiles, per_tile), 1)
        < face_count[0]
    ).astype(jnp.float32)
    local_weight = is_local_tiled.astype(jnp.float32)
    normal_tiled = face_normal.reshape(3, tiles, per_tile)

    def ghosts(vector_in):
        outgoing = (
            jnp.stack(
                [jnp.take(vector_in, send_list[which], axis=1) for which in range(list_total)]
            )
            * keep_mask[:, None, :]
        )
        incoming = jnp.stack(
            [
                passed_along(outgoing[which], "cells", shift_list[which])
                for which in range(list_total)
            ]
        )
        return jnp.transpose(incoming, (1, 0, 2)).reshape(vector_in.shape[0], halo_total)

    def to_faces(vector_in):
        rows = vector_in.shape[0]
        blocks = vector_in.reshape(rows, tiles, 128)
        paired = jnp.concatenate([blocks, jnp.roll(blocks, -1, axis=1)], axis=2)
        halo_cells = ghosts(vector_in)
        halo_windows = halo_cells.reshape(rows, window_count, window)[:, window_pick]
        left_side = jnp.einsum("tfc,btc->btf", owner_hot, blocks, precision=highest)
        right_side = jnp.einsum("tfc,btc->btf", local_hot, paired, precision=highest)
        right_side = right_side + jnp.einsum(
            "tfc,btc->btf", halo_hot, halo_windows, precision=highest
        )
        return (left_side, right_side)

    def to_cells(owner_values, neighbour_values):
        rows = owner_values.shape[0]
        owned = jnp.einsum("tfc,btf->btc", owner_hot, owner_values, precision=highest)
        beside = jnp.einsum("tfc,btf->btc", local_hot, neighbour_values, precision=highest)
        summed = owned + beside[:, :, :128] + jnp.roll(beside[:, :, 128:], 1, axis=1)
        return summed.reshape(rows, cells_here)

    left_state, right_state = to_faces(flow_state)
    normal_speed = 0.5 * jnp.sum(normal_tiled * (left_state[:3] + right_state[:3]), axis=0)
    normal_size = jnp.sqrt(jnp.sum(normal_tiled * normal_tiled, axis=0))
    wave_speed = jnp.abs(normal_speed) + 2.0 * normal_size
    owner_terms = (
        0.5
        * jnp.concatenate([normal_speed[None], normal_tiled, wave_speed[None]], axis=0)
        * is_live
    )
    neighbour_terms = jnp.concatenate(
        [-0.5 * normal_speed[None], -0.5 * normal_tiled, 0.5 * wave_speed[None]], axis=0
    ) * (is_live * local_weight)
    block_terms = lax.psum(to_cells(owner_terms, neighbour_terms), "faces")
    velocity_diag = volume_rate + block_terms[0] + block_terms[4]
    pressure_diag = volume_rate + block_terms[4]
    coupling = block_terms[1:4]
    schur = pressure_diag - jnp.sum(coupling * coupling, axis=0) / velocity_diag

    def precondition(vector_in):
        pressure = (
            vector_in[3] - jnp.sum(coupling * vector_in[:3], axis=0) / velocity_diag
        ) / schur
        velocity = (vector_in[:3] - coupling * pressure) / velocity_diag
        return jnp.concatenate([velocity, pressure[None]], axis=0)

    def apply_matrix(vector_in):
        left_side, right_side = to_faces(vector_in)
        face_sum = left_side + right_side
        central = jnp.concatenate(
            [
                normal_speed * face_sum[:3] + normal_tiled * face_sum[3],
                jnp.sum(normal_tiled * face_sum[:3], axis=0)[None],
            ],
            axis=0,
        )
        face_flux = (0.5 * central - 0.5 * wave_speed * (right_side - left_side)) * is_live
        partial_value = to_cells(face_flux, -face_flux * local_weight)
        return volume_rate * vector_in + lax.psum(partial_value, "faces")

    solution_field = jnp.zeros_like(source_term)
    residual = source_term
    direction = source_term
    rho_now = lax.psum(jnp.sum(source_term * residual), "cells")
    for iteration in range(ITERS):
        pre_dir = precondition(direction)
        image = apply_matrix(pre_dir)
        step_alpha = rho_now / lax.psum(jnp.sum(source_term * image), "cells")
        middle = residual - step_alpha * image
        pre_mid = precondition(middle)
        second = apply_matrix(pre_mid)
        second_mid, second_sq, shadow_mid, shadow_second = lax.psum(
            (
                jnp.sum(second * middle),
                jnp.sum(second * second),
                jnp.sum(source_term * middle),
                jnp.sum(source_term * second),
            ),
            "cells",
        )
        step_omega = second_mid / second_sq
        solution_field = solution_field + step_alpha * pre_dir + step_omega * pre_mid
        residual = middle - step_omega * second
        rho_next = shadow_mid - step_omega * shadow_second
        if iteration + 1 < ITERS:
            ratio_beta = rho_next / rho_now * (step_alpha / step_omega)
            direction = residual + ratio_beta * (direction - step_omega * image)
            rho_now = rho_next
    return (solution_field, residual)


def solution(mesh):
    in_specs = (
        P(None, "cells"),
        P(None, "cells"),
        P("cells"),
        P(None, ("cells", "faces")),
        P(("cells", "faces")),
        P(("cells", "faces")),
        P(("cells", "faces")),
        P("cells", None),
        P("cells"),
    )
    out_specs = (P(None, "cells"), P(None, "cells"))
    return jax.shard_map(body, mesh=mesh, in_specs=in_specs, out_specs=out_specs, check_vma=False)
```

profile of v0, /device:TPU:0, one launch (start us, length us, event | category | flops | bytes accessed | tf_op | source)
XLA Modules:
  0.0 638.7 jit_solution(4085861947890233693)
XLA Ops:
  42.0 6.4 fusion.61
  54.7 6.8 %fusion.4 = f32[64,4,192]{2,1,0:T(4,128)S(1)} fusion(s32[64,192]{1,0:T(8,128)S(1)} %get-tuple-element.48, f32[64,4,256]{2,1,0:T(4,128)S(1)} %gather_fusion), kind=kOutput, calls=%fused_computation.40 | convolution fusion | flops 154140672 | bytes 507904 | tf_op jit(solution)/shard_map/tfc,btc->btf/dot_general | solution.py:93
  61.5 6.9 %fusion.56 = f32[4,64,192]{2,0,1:T(4,128)S(1)} fusion(f32[64,4,192]{2,1,0:T(4,128)S(1)} %fusion.4, s32[64,192]{1,0:T(8,128)S(1)} %get-tuple-element.47, f32[4,1,128]{2,0,1:T(4,128)S(1)} %slice.454, f32[4,63,128]{2,0,1:T(4,128)S(1)} %slice.453, f32[4,64,128]{2,0,1:T(4,128)S(1)} %bitcast.444), kind=kOutput, calls=%fused_computation.94 | convolution fusion | flops 154320896 | bytes 704512 | tf_op jit(solution)/shard_map/tfc,btc->btf/dot_general | solution.py:92
  68.8 6.9 %fusion.50 = f32[5,64,256]{2,0,1:T(8,128)S(1)} fusion(s32[64,192]{1,0:T(8,128)S(1)} %get-tuple-element.47, f32[5,64,192]{2,1,0:T(8,128)S(1)} %maximum_multiply_fusion.1), kind=kOutput, calls=%fused_computation.88 | convolution fusion | flops 191889408 | bytes 622592 | tf_op jit(solution)/shard_map/tfc,btf->btc/dot_general | solution.py:101
  75.7 5.4 fusion.54
  81.3 18.1 %all-reduce.9.cloned.1.call-done = f32[5,8192]{1,0:T(8,128)} async-done(((f32[5,8192]{1,0:T(8,128)}), f32[5,8192]{1,0:T(8,128)}) %all-reduce.9.cloned.1.call-update) | async-done | bytes 163856 | tf_op jit(solution)/shard_map/psum | solution.py:117
  122.9 6.4 fusion.37
  145.3 6.8 %fusion.3 = f32[64,4,192]{2,1,0:T(4,128)S(1)} fusion(s32[64,192]{1,0:T(8,128)S(1)} %get-tuple-element.48, f32[64,4,256]{2,1,0:T(4,128)S(1)} %gather_fusion.1), kind=kOutput, calls=%fused_computation.39 | convolution fusion | flops 154140672 | bytes 507904 | tf_op jit(solution)/shard_map/tfc,btc->btf/dot_general | solution.py:93
  152.1 6.9 %fusion.57 = f32[64,4,192]{2,1,0:T(4,128)S(1)} fusion(f32[64,4,192]{2,1,0:T(4,128)S(1)} %fusion.3, s32[64,192]{1,0:T(8,128)S(1)} %get-tuple-element.47, f32[4,1,128]{2,0,1:T(4,128)S(1)} %fusion.167, f32[4,63,128]{2,0,1:T(4,128)S(1)} %fusion.154, f32[1,64,128]{2,0,1:T(1,128)S(1)} %bitcast.425, f32[3,64,128]{2,0,1:T(4,128)S(1)} %bitcast.399), kind=kOutput, calls=%fused_computation.95 | convolution fusion | flops 154386432 | bytes 704512 | tf_op jit(solution)/shard_map/tfc,btc->btf/dot_general | solution.py:92
  165.1 5.4 fusion.81
  170.6 17.9 %all-reduce.11.cloned.1.call-done = f32[4,8192]{1,0:T(4,128)} async-done(((f32[4,8192]{1,0:T(4,128)}), f32[4,8192]{1,0:T(4,128)}) %all-reduce.11.cloned.1.call-update) | async-done | bytes 131088 | tf_op jit(solution)/shard_map/psum | solution.py:142
  190.2 42.6 %all-reduce.2 = (f32[]{:T(128)}, f32[]{:T(128)}) all-reduce(f32[]{:T(128)} %get-tuple-element.16, f32[]{:T(128)} %get-tuple-element.15), channel_id=1, replica_groups=mesh['cells'=16,'faces'=2] {'cells'}, use_global_device_ids=true, to_apply=%region_1.2 | all-reduce | flops 2 | bytes 16 | tf_op jit(solution)/shard_map/psum | solution.py:147
  254.6 6.4 fusion.35
  262.4 5.6 collective-permute-start.15
  275.2 6.8 %fusion.2 = f32[64,4,192]{2,1,0:T(4,128)S(1)} fusion(s32[64,192]{1,0:T(8,128)S(1)} %get-tuple-element.48, f32[64,4,256]{2,1,0:T(4,128)S(1)} %gather_fusion.2), kind=kOutput, calls=%fused_computation.38 | convolution fusion | flops 154140672 | bytes 507904 | tf_op jit(solution)/shard_map/tfc,btc->btf/dot_general | solution.py:93
  282.0 6.9 %fusion.58 = f32[64,4,192]{2,1,0:T(4,128)S(1)} fusion(f32[64,4,192]{2,1,0:T(4,128)S(1)} %fusion.2, s32[64,192]{1,0:T(8,128)S(1)} %get-tuple-element.47, f32[4,1,128]{2,0,1:T(4,128)S(1)} %fusion.166, f32[4,63,128]{2,0,1:T(4,128)S(1)} %fusion.153, f32[1,64,128]{2,0,1:T(1,128)S(1)} %bitcast.432, f32[3,64,128]{2,0,1:T(4,128)S(1)} %bitcast.403), kind=kOutput, calls=%fused_computation.96 | convolution fusion | flops 154386432 | bytes 704512 | tf_op jit(solution)/shard_map/tfc,btc->btf/dot_general | solution.py:92
  295.0 5.4 fusion.78
  300.5 18.5 %all-reduce.13.cloned.1.call-done = f32[4,8192]{1,0:T(4,128)} async-done(((f32[4,8192]{1,0:T(4,128)}), f32[4,8192]{1,0:T(4,128)}) %all-reduce.13.cloned.1.call-update) | async-done | bytes 131088 | tf_op jit(solution)/shard_map/psum | solution.py:142
  320.7 42.9 %all-reduce.1 = (f32[]{:T(128)}, f32[]{:T(128)}, f32[]{:T(128)}, f32[]{:T(128)}) all-reduce(f32[]{:T(128)} %get-tuple-element.14, f32[]{:T(128)} %get-tuple-element.13, f32[]{:T(128)} %get-tuple-element.12, f32[]{:T(128)} %get-tuple-element.11), channel_id=1, replica_groups=mesh['cells'=16,'faces'=2] {'cells'}, use_global_device_ids=true, to_apply=%region_19.21 | all-reduce | flops 4 | bytes 32 | tf_op jit(solution)/shard_map/psum | solution.py:155
  389.9 6.4 fusion.33
  397.7 5.6 collective-permute-start.21
  410.5 6.8 %fusion.1 = f32[64,4,192]{2,1,0:T(4,128)S(1)} fusion(s32[64,192]{1,0:T(8,128)S(1)} %get-tuple-element.48, f32[64,4,256]{2,1,0:T(4,128)S(1)} %gather_fusion.3), kind=kOutput, calls=%fused_computation.37 | convolution fusion | flops 154140672 | bytes 507904 | tf_op jit(solution)/shard_map/tfc,btc->btf/dot_general | solution.py:93
  417.3 6.9 %fusion.59 = f32[64,4,192]{2,1,0:T(4,128)S(1)} fusion(f32[64,4,192]{2,1,0:T(4,128)S(1)} %fusion.1, s32[64,192]{1,0:T(8,128)S(1)} %get-tuple-element.47, f32[4,1,128]{2,0,1:T(4,128)S(1)} %fusion.165, f32[4,63,128]{2,0,1:T(4,128)S(1)} %fusion.152, f32[1,64,128]{2,0,1:T(1,128)S(1)} %bitcast.417, f32[3,64,128]{2,0,1:T(4,128)S(1)} %bitcast.395), kind=kOutput, calls=%fused_computation.97 | convolution fusion | flops 154386432 | bytes 704512 | tf_op jit(solution)/shard_map/tfc,btc->btf/dot_general | solution.py:92
  430.3 5.4 fusion.75
  435.8 18.5 %all-reduce.15.cloned.1.call-done = f32[4,8192]{1,0:T(4,128)} async-done(((f32[4,8192]{1,0:T(4,128)}), f32[4,8192]{1,0:T(4,128)}) %all-reduce.15.cloned.1.call-update) | async-done | bytes 131088 | tf_op jit(solution)/shard_map/psum | solution.py:142
  455.9 42.6 %psum.108 = f32[]{:T(128)} all-reduce(f32[]{:T(128)} %multiply_reduce_fusion.4), channel_id=1, replica_groups=mesh['cells'=16,'faces'=2] {'cells'}, use_global_device_ids=true, to_apply=%region_26.28 | all-reduce | flops 1 | bytes 8 | tf_op jit(solution)/shard_map/psum | solution.py:151
  520.7 6.4 fusion.31
  528.5 5.6 collective-permute-start.27
  541.3 6.8 %fusion = f32[64,4,192]{2,1,0:T(4,128)S(1)} fusion(s32[64,192]{1,0:T(8,128)S(1)} %get-tuple-element.48, f32[64,4,256]{2,1,0:T(4,128)S(1)} %gather_fusion.4), kind=kOutput, calls=%fused_computation.36 | convolution fusion | flops 154140672 | bytes 507904 | tf_op jit(solution)/shard_map/tfc,btc->btf/dot_general | solution.py:93
  548.1 6.9 %fusion.60 = f32[64,4,192]{2,1,0:T(4,128)S(1)} fusion(f32[64,4,192]{2,1,0:T(4,128)S(1)} %fusion, s32[64,192]{1,0:T(8,128)S(1)} %get-tuple-element.47, f32[4,1,128]{2,0,1:T(4,128)S(1)} %fusion.164, f32[4,63,128]{2,0,1:T(4,128)S(1)} %fusion.151, f32[1,64,128]{2,0,1:T(1,128)S(1)} %bitcast.439, f32[3,64,128]{2,0,1:T(4,128)S(1)} %bitcast.407), kind=kOutput, calls=%fused_computation.98 | convolution fusion | flops 154386432 | bytes 704512 | tf_op jit(solution)/shard_map/tfc,btc->btf/dot_general | solution.py:92
  566.5 18.6 %all-reduce.17.cloned.1.call-done = f32[4,8192]{1,0:T(4,128)} async-done(((f32[4,8192]{1,0:T(4,128)}), f32[4,8192]{1,0:T(4,128)}) %all-reduce.17.cloned.1.call-update) | async-done | bytes 131088 | tf_op jit(solution)/shard_map/psum | solution.py:142
  586.7 42.6 %all-reduce = (f32[]{:T(128)}, f32[]{:T(128)}) all-reduce(f32[]{:T(128)} %get-tuple-element.10, f32[]{:T(128)} %get-tuple-element.9), channel_id=1, replica_groups=mesh['cells'=16,'faces'=2] {'cells'}, use_global_device_ids=true, to_apply=%region_31.33 | all-reduce | flops 2 | bytes 16 | tf_op jit(solution)/shard_map/psum | solution.py:155
  (373 shorter events, 206.0 us)
Async XLA Ops:
  7.2 92.2 %all-reduce.9.cloned.1.call-start = ((), (), s32[]{:S(2)}) async-start(), calls=%async_computation | async-start | bytes 524288 | tf_op jit(solution)/shard_map/psum | solution.py:117
  30.6 18.8 %collective-permute-start = (f32[4,256]{1,0:T(4,128)S(1)}, f32[4,256]{1,0:T(4,128)S(1)}, u32[]{:S(2)}, u32[]{:S(2)}) collective-permute-start(f32[4,256]{1,0:T(4,128)S(1)} %get-tuple-element.78), channel_id=1, source_target_pairs={{30,0},{0,2},{2,4},{4,6},{6,8},{8,10},{10,12},{12,14},{14,16},{16,... | collective-permute-start | bytes 12296 | tf_op jit(solution)/shard_map/ppermute | solution.py:13
  33.7 17.1 %collective-permute-start.1 = (f32[4,256]{1,0:T(4,128)S(1)}, f32[4,256]{1,0:T(4,128)S(1)}, u32[]{:S(2)}, u32[]{:S(2)}) collective-permute-start(f32[4,256]{1,0:T(4,128)S(1)} %get-tuple-element.77), channel_id=1, source_target_pairs={{28,0},{30,2},{0,4},{2,6},{4,8},{6,10},{8,12},{10,14},{12,16},{14,... | collective-permute-start | bytes 12296 | tf_op jit(solution)/shard_map/ppermute | solution.py:13
  35.2 15.6 %collective-permute-start.2 = (f32[4,256]{1,0:T(4,128)S(1)}, f32[4,256]{1,0:T(4,128)S(1)}, u32[]{:S(2)}, u32[]{:S(2)}) collective-permute-start(f32[4,256]{1,0:T(4,128)S(1)} %get-tuple-element.76), channel_id=1, source_target_pairs={{26,0},{28,2},{30,4},{0,6},{2,8},{4,10},{6,12},{8,14},{10,16},{12,... | collective-permute-start | bytes 12296 | tf_op jit(solution)/shard_map/ppermute | solution.py:13
  37.6 13.2 %collective-permute-start.3 = (f32[4,256]{1,0:T(4,128)S(1)}, f32[4,256]{1,0:T(4,128)S(1)}, u32[]{:S(2)}, u32[]{:S(2)}) collective-permute-start(f32[4,256]{1,0:T(4,128)S(1)} %get-tuple-element.75), channel_id=1, source_target_pairs={{2,0},{4,2},{6,4},{8,6},{10,8},{12,10},{14,12},{16,14},{18,16},{20... | collective-permute-start | bytes 12296 | tf_op jit(solution)/shard_map/ppermute | solution.py:13
  40.9 10.0 %collective-permute-start.4 = (f32[4,256]{1,0:T(4,128)S(1)}, f32[4,256]{1,0:T(4,128)S(1)}, u32[]{:S(2)}, u32[]{:S(2)}) collective-permute-start(f32[4,256]{1,0:T(4,128)S(1)} %get-tuple-element.74), channel_id=1, source_target_pairs={{4,0},{6,2},{8,4},{10,6},{12,8},{14,10},{16,12},{18,14},{20,16},{2... | collective-permute-start | bytes 12296 | tf_op jit(solution)/shard_map/ppermute | solution.py:13
  49.4 4.6 collective-permute-start.5
  81.2 107.4 %all-reduce.11.cloned.1.call-start = ((), (), s32[]{:S(2)}) async-start(), calls=%async_computation.1 | async-start | bytes 262144 | tf_op jit(solution)/shard_map/psum | solution.py:142
  130.6 9.5 %collective-permute-start.6 = (f32[4,256]{1,0:T(4,128)S(1)}, f32[4,256]{1,0:T(4,128)S(1)}, u32[]{:S(2)}, u32[]{:S(2)}) collective-permute-start(f32[4,256]{1,0:T(4,128)S(1)} %get-tuple-element.72), channel_id=1, source_target_pairs={{30,0},{0,2},{2,4},{4,6},{6,8},{8,10},{10,12},{12,14},{14,16},{16,... | collective-permute-start | bytes 12296 | tf_op jit(solution)/shard_map/ppermute | solution.py:13
  132.4 8.8 %collective-permute-start.7 = (f32[4,256]{1,0:T(4,128)S(1)}, f32[4,256]{1,0:T(4,128)S(1)}, u32[]{:S(2)}, u32[]{:S(2)}) collective-permute-start(f32[4,256]{1,0:T(4,128)S(1)} %get-tuple-element.71), channel_id=1, source_target_pairs={{28,0},{30,2},{0,4},{2,6},{4,8},{6,10},{8,12},{10,14},{12,16},{14,... | collective-permute-start | bytes 12296 | tf_op jit(solution)/shard_map/ppermute | solution.py:13
  133.9 7.3 %collective-permute-start.8 = (f32[4,256]{1,0:T(4,128)S(1)}, f32[4,256]{1,0:T(4,128)S(1)}, u32[]{:S(2)}, u32[]{:S(2)}) collective-permute-start(f32[4,256]{1,0:T(4,128)S(1)} %get-tuple-element.70), channel_id=1, source_target_pairs={{26,0},{28,2},{30,4},{0,6},{2,8},{4,10},{6,12},{8,14},{10,16},{12,... | collective-permute-start | bytes 12296 | tf_op jit(solution)/shard_map/ppermute | solution.py:13
  136.3 5.0 collective-permute-start.9
  140.1 4.5 collective-permute-start.11
  170.6 148.4 %all-reduce.13.cloned.1.call-start = ((), (), s32[]{:S(2)}) async-start(), calls=%async_computation.2 | async-start | bytes 262144 | tf_op jit(solution)/shard_map/psum | solution.py:142
  262.2 7.7 %collective-permute-start.12 = (f32[4,256]{1,0:T(4,128)S(1)}, f32[4,256]{1,0:T(4,128)S(1)}, u32[]{:S(2)}, u32[]{:S(2)}) collective-permute-start(f32[4,256]{1,0:T(4,128)S(1)} %get-tuple-element.66), channel_id=1, source_target_pairs={{30,0},{0,2},{2,4},{4,6},{6,8},{8,10},{10,12},{12,14},{14,16},{16,... | collective-permute-start | bytes 12296 | tf_op jit(solution)/shard_map/ppermute | solution.py:13
  262.3 10.6 %collective-permute-start.13 = (f32[4,256]{1,0:T(4,128)S(1)}, f32[4,256]{1,0:T(4,128)S(1)}, u32[]{:S(2)}, u32[]{:S(2)}) collective-permute-start(f32[4,256]{1,0:T(4,128)S(1)} %get-tuple-element.65), channel_id=1, source_target_pairs={{28,0},{30,2},{0,4},{2,6},{4,8},{6,10},{8,12},{10,14},{12,16},{14,... | collective-permute-start | bytes 12296 | tf_op jit(solution)/shard_map/ppermute | solution.py:13
  262.4 10.5 %collective-permute-start.14 = (f32[4,256]{1,0:T(4,128)S(1)}, f32[4,256]{1,0:T(4,128)S(1)}, u32[]{:S(2)}, u32[]{:S(2)}) collective-permute-start(f32[4,256]{1,0:T(4,128)S(1)} %get-tuple-element.64), channel_id=1, source_target_pairs={{26,0},{28,2},{30,4},{0,6},{2,8},{4,10},{6,12},{8,14},{10,16},{12,... | collective-permute-start | bytes 12296 | tf_op jit(solution)/shard_map/ppermute | solution.py:13
  262.4 10.5 %collective-permute-start.15 = (f32[4,256]{1,0:T(4,128)S(1)}, f32[4,256]{1,0:T(4,128)S(1)}, u32[]{:S(2)}, u32[]{:S(2)}) collective-permute-start(f32[4,256]{1,0:T(4,128)S(1)} %get-tuple-element.63), channel_id=1, source_target_pairs={{2,0},{4,2},{6,4},{8,6},{10,8},{12,10},{14,12},{16,14},{18,16},{20... | collective-permute-start | bytes 12296 | tf_op jit(solution)/shard_map/ppermute | solution.py:13
  268.0 4.9 collective-permute-start.16
  300.4 153.8 %all-reduce.15.cloned.1.call-start = ((), (), s32[]{:S(2)}) async-start(), calls=%async_computation.3 | async-start | bytes 262144 | tf_op jit(solution)/shard_map/psum | solution.py:142
  397.5 7.7 %collective-permute-start.18 = (f32[4,256]{1,0:T(4,128)S(1)}, f32[4,256]{1,0:T(4,128)S(1)}, u32[]{:S(2)}, u32[]{:S(2)}) collective-permute-start(f32[4,256]{1,0:T(4,128)S(1)} %get-tuple-element.60), channel_id=1, source_target_pairs={{30,0},{0,2},{2,4},{4,6},{6,8},{8,10},{10,12},{12,14},{14,16},{16,... | collective-permute-start | bytes 12296 | tf_op jit(solution)/shard_map/ppermute | solution.py:13
  397.6 10.6 %collective-permute-start.19 = (f32[4,256]{1,0:T(4,128)S(1)}, f32[4,256]{1,0:T(4,128)S(1)}, u32[]{:S(2)}, u32[]{:S(2)}) collective-permute-start(f32[4,256]{1,0:T(4,128)S(1)} %get-tuple-element.59), channel_id=1, source_target_pairs={{28,0},{30,2},{0,4},{2,6},{4,8},{6,10},{8,12},{10,14},{12,16},{14,... | collective-permute-start | bytes 12296 | tf_op jit(solution)/shard_map/ppermute | solution.py:13
  397.7 10.5 %collective-permute-start.20 = (f32[4,256]{1,0:T(4,128)S(1)}, f32[4,256]{1,0:T(4,128)S(1)}, u32[]{:S(2)}, u32[]{:S(2)}) collective-permute-start(f32[4,256]{1,0:T(4,128)S(1)} %get-tuple-element.58), channel_id=1, source_target_pairs={{26,0},{28,2},{30,4},{0,6},{2,8},{4,10},{6,12},{8,14},{10,16},{12,... | collective-permute-start | bytes 12296 | tf_op jit(solution)/shard_map/ppermute | solution.py:13
  397.7 10.5 %collective-permute-start.21 = (f32[4,256]{1,0:T(4,128)S(1)}, f32[4,256]{1,0:T(4,128)S(1)}, u32[]{:S(2)}, u32[]{:S(2)}) collective-permute-start(f32[4,256]{1,0:T(4,128)S(1)} %get-tuple-element.57), channel_id=1, source_target_pairs={{2,0},{4,2},{6,4},{8,6},{10,8},{12,10},{14,12},{16,14},{18,16},{20... | collective-permute-start | bytes 12296 | tf_op jit(solution)/shard_map/ppermute | solution.py:13
  403.3 4.9 collective-permute-start.22
  435.7 149.3 %all-reduce.17.cloned.1.call-start = ((), (), s32[]{:S(2)}) async-start(), calls=%async_computation.4 | async-start | bytes 262144 | tf_op jit(solution)/shard_map/psum | solution.py:142
  528.3 7.7 %collective-permute-start.24 = (f32[4,256]{1,0:T(4,128)S(1)}, f32[4,256]{1,0:T(4,128)S(1)}, u32[]{:S(2)}, u32[]{:S(2)}) collective-permute-start(f32[4,256]{1,0:T(4,128)S(1)} %get-tuple-element.54), channel_id=1, source_target_pairs={{30,0},{0,2},{2,4},{4,6},{6,8},{8,10},{10,12},{12,14},{14,16},{16,... | collective-permute-start | bytes 12296 | tf_op jit(solution)/shard_map/ppermute | solution.py:13
  528.4 10.6 %collective-permute-start.25 = (f32[4,256]{1,0:T(4,128)S(1)}, f32[4,256]{1,0:T(4,128)S(1)}, u32[]{:S(2)}, u32[]{:S(2)}) collective-permute-start(f32[4,256]{1,0:T(4,128)S(1)} %get-tuple-element.53), channel_id=1, source_target_pairs={{28,0},{30,2},{0,4},{2,6},{4,8},{6,10},{8,12},{10,14},{12,16},{14,... | collective-permute-start | bytes 12296 | tf_op jit(solution)/shard_map/ppermute | solution.py:13
  528.5 10.5 %collective-permute-start.26 = (f32[4,256]{1,0:T(4,128)S(1)}, f32[4,256]{1,0:T(4,128)S(1)}, u32[]{:S(2)}, u32[]{:S(2)}) collective-permute-start(f32[4,256]{1,0:T(4,128)S(1)} %get-tuple-element.52), channel_id=1, source_target_pairs={{26,0},{28,2},{30,4},{0,6},{2,8},{4,10},{6,12},{8,14},{10,16},{12,... | collective-permute-start | bytes 12296 | tf_op jit(solution)/shard_map/ppermute | solution.py:13
  528.5 10.5 %collective-permute-start.27 = (f32[4,256]{1,0:T(4,128)S(1)}, f32[4,256]{1,0:T(4,128)S(1)}, u32[]{:S(2)}, u32[]{:S(2)}) collective-permute-start(f32[4,256]{1,0:T(4,128)S(1)} %get-tuple-element.51), channel_id=1, source_target_pairs={{2,0},{4,2},{6,4},{8,6},{10,8},{12,10},{14,12},{16,14},{18,16},{20... | collective-permute-start | bytes 12296 | tf_op jit(solution)/shard_map/ppermute | solution.py:13
  534.1 4.9 collective-permute-start.28
  536.0 4.5 collective-permute-start.29
  (12 other events, 352.0 us)
Sparse Core Ops, SparseCore 0:
  81.3 18.0 all-reduce.8
  170.7 17.8 all-reduce.10
  300.5 18.3 all-reduce.12
  435.8 18.3 all-reduce.14
  566.6 18.3 all-reduce.16
where the time goes:
time: 640 us; the launch traced here: 639 us
  blocking collectives  171 us (27%)
  matrix products  155 us (24%)
  local copies, waits for them, and re-layouts  111 us (17%)
  waiting for transfers between devices  103 us (16%)
  starting transfers between devices  54.7 us (9%)
  between operations  24.9 us (4%)
  other arithmetic  19.9 us (3%)
    gather x30, local copies, waits for them, and re-layouts, ghosts(): jnp.take(vector_in, send_list[which], axis=1)  87.3 us
    psum x2, blocking collectives, body(): lax.psum((jnp.sum(second * middle), jnp.sum(second * second), jnp.sum(sou...  85.5 us
    psum x4, waiting for transfers between devices, apply_matrix(): return volume_rate * vector_in + lax.psum(partial_value, 'faces')  73.5 us
    ppermute x30, starting transfers between devices, passed_along(): return lax.ppermute(block, axis, route)  54.5 us
    psum x1, blocking collectives, body(): rho_now = lax.psum(jnp.sum(source_term * residual), 'cells')  42.6 us
    psum x1, blocking collectives, body(): step_alpha = rho_now / lax.psum(jnp.sum(source_term * image), 'cells')  42.6 us
    dot_general x5, matrix products, to_faces(): jnp.einsum('tfc,btc->btf', local_hot, paired, precision=highest)  34.4 us
    dot_general x5, matrix products, to_faces(): jnp.einsum('tfc,btc->btf', halo_hot, halo_windows, precision=highest)  34 us
  transfers between devices with their start and end apart: 35, of which 11 were waited for; matrix products, arithmetic and copies ran while one was open for 1% of the time, Pallas kernels for 0%

commit v1 on v0

v1 whole, which is shorter than its diff:
```python
import functools

import jax
import jax.numpy as jnp
from jax import lax
from jax.experimental import pallas as pl
from jax.experimental.pallas import tpu as pltpu
from jax.sharding import PartitionSpec as P

ITERS = 2
LANES = 128
MESH = pl.DeviceIdType.MESH
F32 = jnp.float32
BF16 = jnp.bfloat16


def take_lanes(source, index):
    return jnp.take_along_axis(source, index, axis=1, mode="promise_in_bounds")


def split(value):
    high = value.astype(BF16).astype(F32)
    return high, value - high


def kernel(
    parts,
    cores,
    count_ref,
    flow_ref,
    source_ref,
    volume_ref,
    normal_ref,
    owner_ref,
    neighbour_ref,
    list_ref,
    halo_count_ref,
    solution_ref,
    residual_ref,
    own_lane,
    right_lane,
    right_kind,
    own_row,
    local_row,
    face_u,
    face_s,
    face_n,
    signed_hot,
    plain_hot,
    flux_rows,
    size_rows,
    cell_rows,
    size_cells,
    fields,
    halo_rows,
    blocks,
    vecs,
    pair_out,
    pair_in,
    halo_out,
    halo_in,
    dot_out,
    dot_in,
    pair_send,
    pair_recv,
    halo_send,
    halo_recv,
    dot_send,
    dot_recv,
):
    me = lax.axis_index("cells")
    core = lax.axis_index("faces")
    other = (core + 1) % cores
    tiles = volume_ref.shape[0]
    pairs = tiles // 2
    groups = pairs // 8
    cells = tiles * LANES
    lists = halo_in.shape[1]
    lists_here = lists // cores
    width = list_ref.shape[2] * list_ref.shape[1]

    barrier = pltpu.get_barrier_semaphore()
    for step in range(1, parts * cores):
        number = (me * cores + core + step) % (parts * cores)
        pl.semaphore_signal(
            barrier,
            inc=1,
            device_id={"cells": number // cores, "faces": number % cores},
            device_id_type=MESH,
        )

    lane = lax.broadcasted_iota(jnp.int32, (pairs, LANES), 1)
    pair_id = lax.broadcasted_iota(jnp.int32, (pairs, LANES), 0)
    late = lane >= LANES // 2
    count = count_ref[0]
    for j in range(3):
        tile = 2 * pair_id + (0 if j == 0 else 1)
        if j == 1:
            tile = 2 * pair_id + late.astype(jnp.int32)
        owner = owner_ref[pl.ds(j, pairs, stride=3), :]
        beside = neighbour_ref[pl.ds(j, pairs, stride=3), :]
        live = (3 * pair_id + j) * LANES + lane < count
        is_local = beside < cells
        column = beside - tile * LANES
        column = jnp.where(column < 0, column + cells, column)
        slot = beside - cells - (tile % lists) * width
        place = jnp.where(is_local, column, slot)
        upper = place >= LANES
        own = owner - tile * LANES
        own_lane[j] = own
        right_lane[j] = jnp.where(upper, place - LANES, place)
        right_kind[j] = jnp.where(is_local, 0, 2) + upper.astype(jnp.int32)
        own_row[j] = jnp.where(live, own, -1)
        local_row[j] = jnp.where(live & is_local, column, -1)

    def start_halo(turn, field):
        row8 = lax.broadcasted_iota(jnp.int32, (8, LANES), 0)
        for i in range(lists_here):
            which = core * lists_here + i
            rows = []
            wanted = list_ref[which]
            limit = halo_count_ref[which]
            for b in range(4):
                for half in range(2):
                    cell = jnp.broadcast_to(wanted[half : half + 1], (8, LANES))
                    row = cell // LANES
                    col = cell - row * LANES
                    found = jnp.zeros((8, LANES), F32)
                    for g in range(tiles // 8):
                        got = take_lanes(field(b, g), col)
                        found = jnp.where(row == row8 + 8 * g, got, found)
                    found = jnp.sum(found, axis=0, keepdims=True)
                    used = (
                        lax.broadcasted_iota(jnp.int32, (1, LANES), 1) + half * LANES < limit
                    )
                    rows.append(jnp.where(used, found, 0.0))
            halo_out[turn, i] = jnp.concatenate(rows, axis=0)
        for i in range(lists_here):
            target = (me + (1 - 2 * core) * (i + 1) + parts) % parts
            for c in range(cores):
                pltpu.make_async_remote_copy(
                    src_ref=halo_out.at[turn, i],
                    dst_ref=halo_in.at[turn, core * lists_here + i],
                    send_sem=halo_send.at[turn],
                    recv_sem=halo_recv.at[turn],
                    device_id={"cells": target, "faces": c},
                    device_id_type=MESH,
                ).start()

    def wait_halo(turn):
        pltpu.make_async_copy(halo_in.at[turn], halo_in.at[turn], halo_recv.at[turn]).wait()
        return [halo_in[turn, k] for k in range(lists)]

    def start_pair(turn, rows):
        copy = pltpu.make_async_remote_copy(
            src_ref=pair_out.at[turn, pl.ds(0, rows)],
            dst_ref=pair_in.at[turn, pl.ds(0, rows)],
            send_sem=pair_send.at[turn],
            recv_sem=pair_recv.at[turn],
            device_id={"cells": me, "faces": other},
            device_id_type=MESH,
        )
        copy.start()
        return copy

    def start_dots(turn, partials):
        rows = [
            jnp.sum(p.reshape(tiles // 8, 8, LANES).sum(axis=0), axis=0, keepdims=True)
            for p in partials
        ]
        rows.append(jnp.zeros((8 - len(rows), LANES), F32))
        packed = jnp.concatenate(rows, axis=0)
        dot_out[turn] = packed
        dot_in[turn, me] = packed
        for step in range(1, parts):
            pltpu.make_async_remote_copy(
                src_ref=dot_out.at[turn],
                dst_ref=dot_in.at[turn, me],
                send_sem=dot_send.at[turn],
                recv_sem=dot_recv.at[turn],
                device_id={"cells": (me + step) % parts, "faces": core},
                device_id_type=MESH,
            ).start()

    def wait_dots(turn, number):
        part = dot_in.at[turn, pl.ds(0, parts - 1)]
        pltpu.make_async_copy(part, part, dot_recv.at[turn]).wait()
        total = dot_in[turn, 0]
        for q in range(1, parts):
            total = total + dot_in[turn, q]
        total = jnp.sum(total, axis=1, keepdims=True)
        return [jnp.broadcast_to(total[d : d + 1], (1, LANES)) for d in range(number)]

    def put_field(values, halos):
        for b, value in enumerate(values):
            fields[b, pl.ds(0, tiles), :] = value
            fields[b, pl.ds(tiles, 1), :] = value[0:1]
        period = halo_rows.shape[0] // 8
        for t in range(period):
            halo_rows[pl.ds(t, 8, stride=period), :] = halos[t % lists]

    def sides(g, j, b):
        period = halo_rows.shape[0] // 8
        here = pl.multiple_of(g * 8, 8)
        left_at = own_lane[j, pl.ds(here, 8), :]
        right_at = right_lane[j, pl.ds(here, 8), :]
        kind = right_kind[j, pl.ds(here, 8), :]

        def of_tile(odd):
            first = 16 * g + odd
            halo_first = (16 * g) % lists + odd
            low = fields[b, pl.ds(first, 8, stride=2), :]
            high = fields[b, pl.ds(first + 1, 8, stride=2), :]
            halo_low = halo_rows[pl.ds(2 * b * period + halo_first, 8, stride=2), :]
            halo_high = halo_rows[pl.ds((2 * b + 1) * period + halo_first, 8, stride=2), :]
            left = take_lanes(low, left_at)
            right = jnp.where(
                kind < 2,
                jnp.where(kind == 0, take_lanes(low, right_at), take_lanes(high, right_at)),
                jnp.where(
                    kind == 2, take_lanes(halo_low, right_at), take_lanes(halo_high, right_at)
                ),
            )
            return left, right

        if j == 0:
            return of_tile(0)
        if j == 2:
            return of_tile(1)
        early = lax.broadcasted_iota(jnp.int32, (8, LANES), 1) < LANES // 2
        left_a, right_a = of_tile(0)
        left_b, right_b = of_tile(1)
        return jnp.where(early, left_a, left_b), jnp.where(early, right_a, right_b)

    def put_flux(ref, g, j, b, value):
        high, low = split(value)
        ref[j, pl.ds(64 * g + b, 8, stride=8), :] = high
        ref[j, pl.ds(64 * g + 4 + b, 8, stride=8), :] = low

    def scatter(rows_ref, hot_ref, cells_ref, u):
        start = pl.multiple_of(u * 8, 8)
        for odd in range(2):
            rows = jnp.concatenate(
                [rows_ref[odd, pl.ds(start, 8), :], rows_ref[odd + 1, pl.ds(start, 8), :]], axis=1
            ).astype(BF16)
            result = lax.dot_general(
                rows, hot_ref[2 * u + odd], (((1,), (1,)), ((), ())), preferred_element_type=F32
            )
            at = pl.ds(pl.multiple_of(start * 2 + odd * 8, 8), 8)
            cells_ref[0, at, :] = result[:, :LANES]
            cells_ref[1, at, :] = result[:, LANES:]

    def collect(cells_ref, b):
        def rows(first, side):
            return cells_ref[side, pl.ds(first, tiles, stride=8), :]

        low = rows(b, 0) + rows(4 + b, 0)
        high = rows(b, 1) + rows(4 + b, 1)
        high = jnp.concatenate([high[tiles - 1 :], high[: tiles - 1]], axis=0)
        return low + high

    def apply_matrix(turn, values, halos):
        put_field(values, halos)

        def group(g, carry):
            here = pl.multiple_of(g * 8, 8)
            for j in range(3):
                u = face_u[j, pl.ds(here, 8), :]
                s = face_s[j, pl.ds(here, 8), :]
                n = [face_n[i, j, pl.ds(here, 8), :] for i in range(3)]
                both = [sides(g, j, b) for b in range(4)]
                total = [left + right for left, right in both]
                jump = [s * (right - left) for left, right in both]
                for i in range(3):
                    put_flux(flux_rows, g, j, i, u * total[i] + n[i] * total[3] - jump[i])
                last = n[0] * total[0] + n[1] * total[1] + n[2] * total[2] - jump[3]
                put_flux(flux_rows, g, j, 3, last)
            for i in range(8):
                scatter(flux_rows, signed_hot, cell_rows, g * 8 + i)
            return carry

        lax.fori_loop(0, groups, group, 0)
        mine = [collect(cell_rows, b) for b in range(4)]
        for b in range(4):
            pair_out[turn, b * tiles : (b + 1) * tiles, :] = mine[b]
        copy = start_pair(turn, 4 * tiles)
        copy.wait_recv()
        volume = volume_ref[...]
        return [
            volume * values[b]
            + (
                pair_out[turn, b * tiles : (b + 1) * tiles, :]
                + pair_in[turn, b * tiles : (b + 1) * tiles, :]
            )
            for b in range(4)
        ]

    def precondition(w):
        rvd, rschur = blocks[0], blocks[1]
        n = [blocks[2 + i] for i in range(3)]
        pressure = (w[3] - (n[0] * w[0] + n[1] * w[1] + n[2] * w[2]) * rvd) * rschur
        return [(w[i] - n[i] * pressure) * rvd for i in range(3)] + [pressure]

    def load(which):
        return [vecs[which, b] for b in range(4)]

    def save(which, values):
        for b in range(4):
            vecs[which, b] = values[b]

    def dot(a, b):
        return a[0] * b[0] + a[1] * b[1] + a[2] * b[2] + a[3] * b[3]

    def saved_field(which):
        return lambda b, g: vecs[which, b, 8 * g : 8 * g + 8, :]

    PRE, IMAGE_M, TEMP = 0, 1, 2
    flow = [flow_ref[pl.ds(b, tiles, stride=4), :] for b in range(4)]
    source = [source_ref[pl.ds(b, tiles, stride=4), :] for b in range(4)]
    save(TEMP, flow)
    pl.semaphore_wait(barrier, parts * cores - 1)
    start_halo(0, saved_field(TEMP))
    start_dots(0, [dot(source, source)])

    cell_id = lax.broadcasted_iota(jnp.int32, (2 * LANES, LANES), 0)
    early_row = lax.broadcasted_iota(jnp.int32, (1, LANES), 1) < LANES // 2

    def build(u, carry):
        for odd in range(2):
            for half in range(2):
                j = odd + half
                own = own_row[j, pl.ds(u, 1), :]
                local = local_row[j, pl.ds(u, 1), :]
                if j == 1:
                    keep = early_row if odd == 0 else jnp.logical_not(early_row)
                    own = jnp.where(keep, own, -1)
                    local = jnp.where(keep, local, -1)
                own_hot = jnp.where(cell_id == own, 1.0, 0.0)
                local_hot = jnp.where(cell_id == local, 1.0, 0.0)
                lanes = slice(half * LANES, (half + 1) * LANES)
                signed_hot[2 * u + odd, :, lanes] = (own_hot - local_hot).astype(BF16)
                plain_hot[2 * u + odd, :, lanes] = (own_hot + local_hot).astype(BF16)
        return carry

    lax.fori_loop(0, pairs, build, 0)
    size_rows[...] = jnp.zeros_like(size_rows)

    put_field(flow, wait_halo(0))

    def face_terms(g, carry):
        here = pl.multiple_of(g * 8, 8)
        for j in range(3):
            n = [normal_ref[i, pl.ds(24 * g + j, 8, stride=3), :] for i in range(3)]
            both = [sides(g, j, b) for b in range(3)]
            total = [left + right for left, right in both]
            u = 0.5 * (n[0] * total[0] + n[1] * total[1] + n[2] * total[2])
            s = jnp.abs(u) + 2.0 * jnp.sqrt(n[0] * n[0] + n[1] * n[1] + n[2] * n[2])
            u, s = 0.5 * u, 0.5 * s
            n = [0.5 * n[i] for i in range(3)]
            face_u[j, pl.ds(here, 8), :] = u
            face_s[j, pl.ds(here, 8), :] = s
            put_flux(flux_rows, g, j, 0, u)
            for i in range(3):
                face_n[i, j, pl.ds(here, 8), :] = n[i]
                put_flux(flux_rows, g, j, 1 + i, n[i])
            put_flux(size_rows, g, j, 0, s)
        for i in range(8):
            scatter(flux_rows, signed_hot, cell_rows, g * 8 + i)
            scatter(size_rows, plain_hot, size_cells, g * 8 + i)
        return carry

    lax.fori_loop(0, groups, face_terms, 0)
    for b in range(4):
        pair_out[0, b * tiles : (b + 1) * tiles, :] = collect(cell_rows, b)
    pair_out[0, 4 * tiles : 5 * tiles, :] = collect(size_cells, 0)
    start_pair(0, 5 * tiles).wait_recv()
    sums = [
        pair_out[0, b * tiles : (b + 1) * tiles, :] + pair_in[0, b * tiles : (b + 1) * tiles, :]
        for b in range(5)
    ]
    volume = volume_ref[...]
    rvd = 1.0 / (volume + sums[0] + sums[4])
    coupling = sums[1:4]
    norm = coupling[0] * coupling[0] + coupling[1] * coupling[1] + coupling[2] * coupling[2]
    blocks[0] = rvd
    blocks[1] = 1.0 / (volume + sums[4] - norm * rvd)
    for i in range(3):
        blocks[2 + i] = coupling[i]

    def combine(a, scale, b):
        return [x + scale * y for x, y in zip(a, b)]

    residual = source
    direction = source
    pre_dir = precondition(direction)
    save(PRE, pre_dir)
    start_halo(1, saved_field(PRE))
    (rho,) = wait_dots(0, 1)
    halo_dir = wait_halo(1)
    halo_res = halo_dir
    answer = None
    for iteration in range(ITERS):
        final = iteration + 1 == ITERS
        turn = 1 + 2 * iteration
        image = apply_matrix(turn, pre_dir, halo_dir)
        start_dots(turn, [dot(source, image)])
        pre_image = precondition(image)
        save(IMAGE_M, pre_image)
        start_halo(turn + 1, saved_field(IMAGE_M))
        pre_res = pre_dir if iteration == 0 else precondition(residual)
        (shadow_image,) = wait_dots(turn, 1)
        alpha = rho / shadow_image
        middle = combine(residual, -alpha, image)
        pre_mid = combine(pre_res, -alpha, pre_image)
        halo_image = wait_halo(turn + 1)
        halo_mid = combine(halo_res, -alpha, halo_image)
        second = apply_matrix(turn + 1, pre_mid, halo_mid)
        start_dots(
            turn + 1,
            [dot(second, middle), dot(second, second), dot(source, middle), dot(source, second)],
        )
        if not final:
            pre_second = precondition(second)
            save(TEMP, pre_second)
            start_halo(turn + 2, saved_field(TEMP))
        second_mid, second_sq, shadow_mid, shadow_second = wait_dots(turn + 1, 4)
        omega = second_mid / second_sq
        step = combine([alpha * v for v in pre_dir], omega, pre_mid)
        answer = step if answer is None else [a + s for a, s in zip(answer, step)]
        residual = combine(middle, -omega, second)
        if not final:
            rho_next = shadow_mid - omega * shadow_second
            beta = rho_next / rho * (alpha / omega)
            rho = rho_next
            direction = combine(residual, beta, combine(direction, -omega, image))
            pre_dir = precondition(direction)
            halo_second = wait_halo(turn + 2)
            halo_res = combine(halo_mid, -omega, halo_second)
            halo_dir = combine(halo_res, beta, combine(halo_dir, -omega, halo_image))
    for b in range(4):
        solution_ref[pl.ds(b, tiles, stride=4), :] = answer[b]
        residual_ref[pl.ds(b, tiles, stride=4), :] = residual[b]

    for turn in range(halo_in.shape[0]):
        pltpu.make_async_copy(halo_in.at[turn], halo_in.at[turn], halo_send.at[turn]).wait()
    for turn in range(pair_in.shape[0]):
        part = pair_out.at[turn, pl.ds(0, (5 if turn == 0 else 4) * tiles)]
        pltpu.make_async_copy(part, part, pair_send.at[turn]).wait()
        part = dot_in.at[turn, pl.ds(0, parts - 1)]
        pltpu.make_async_copy(part, part, dot_send.at[turn]).wait()


def body(
    flow_state,
    source_term,
    volume_rate,
    face_normal,
    face_owner,
    face_neighbour,
    face_count,
    send_list,
    halo_count,
):
    parts = lax.axis_size("cells")
    cores = lax.axis_size("faces")
    cells = flow_state.shape[1]
    tiles = cells // LANES
    pairs = tiles // 2
    face_rows = face_owner.shape[0] // LANES
    lists, width = send_list.shape
    period = -(-(lists + 16) // 8) * 8
    turns = 1 + 2 * ITERS

    def by_tile(field):
        return field.reshape(4, tiles, LANES).transpose(1, 0, 2).reshape(4 * tiles, LANES)

    def by_component(field):
        return field.reshape(tiles, 4, LANES).transpose(1, 0, 2).reshape(4, cells)

    vmem = pl.BlockSpec(memory_space=pltpu.VMEM)
    smem = pl.BlockSpec(memory_space=pltpu.SMEM)
    ints = pltpu.VMEM((3, pairs, LANES), jnp.int32)
    floats = pltpu.VMEM((3, pairs, LANES), F32)
    hot = pltpu.VMEM((tiles, 2 * LANES, 2 * LANES), BF16)
    out = jax.ShapeDtypeStruct((4 * tiles, LANES), F32)
    solved, left = pl.pallas_call(
        functools.partial(kernel, parts, cores),
        out_shape=(out, out),
        in_specs=[smem] + [vmem] * 7 + [smem],
        out_specs=(vmem, vmem),
        scratch_shapes=[
            ints,
            ints,
            ints,
            ints,
            ints,
            floats,
            floats,
            pltpu.VMEM((3, 3, pairs, LANES), F32),
            hot,
            hot,
            pltpu.VMEM((3, 8 * pairs, LANES), F32),
            pltpu.VMEM((3, 8 * pairs, LANES), F32),
            pltpu.VMEM((2, 8 * tiles, LANES), F32),
            pltpu.VMEM((2, 8 * tiles, LANES), F32),
            pltpu.VMEM((4, tiles + 8, LANES), F32),
            pltpu.VMEM((8 * period, LANES), F32),
            pltpu.VMEM((5, tiles, LANES), F32),
            pltpu.VMEM((3, 4, tiles, LANES), F32),
            pltpu.VMEM((turns, 5 * tiles, LANES), F32),
            pltpu.VMEM((turns, 5 * tiles, LANES), F32),
            pltpu.VMEM((turns, lists // cores, 8, LANES), F32),
            pltpu.VMEM((turns, lists, 8, LANES), F32),
            pltpu.VMEM((turns, 8, LANES), F32),
            pltpu.VMEM((turns, parts, 8, LANES), F32),
        ]
        + [pltpu.SemaphoreType.DMA((turns,))] * 6,
        compiler_params=pltpu.CompilerParams(
            collective_id=0, has_side_effects=True, vmem_limit_bytes=56 * 1024 * 1024
        ),
    )(
        face_count,
        by_tile(flow_state),
        by_tile(source_term),
        volume_rate.reshape(tiles, LANES),
        face_normal.reshape(3, face_rows, LANES),
        face_owner.reshape(face_rows, LANES),
        face_neighbour.reshape(face_rows, LANES),
        send_list.reshape(lists, width // LANES, LANES),
        halo_count,
    )
    return by_component(solved), by_component(left)


def solution(mesh):
    in_specs = (
        P(None, "cells"),
        P(None, "cells"),
        P("cells"),
        P(None, ("cells", "faces")),
        P(("cells", "faces")),
        P(("cells", "faces")),
        P(("cells", "faces")),
        P("cells", None),
        P("cells"),
    )
    out_specs = (P(None, "cells"), P(None, "cells"))
    return jax.shard_map(body, mesh=mesh, in_specs=in_specs, out_specs=out_specs, check_vma=False)
```

time: 640 us -> 68.2 us (0.11)
  blocking collectives: 171 us -> 0 us
  matrix products: 155 us -> 0 us
  local copies, waits for them, and re-layouts: 111 us -> 4.48 us
  waiting for transfers between devices: 103 us -> 0 us
  Pallas kernels: 0 us -> 62.2 us
  starting transfers between devices: 54.7 us -> 0 us
  between operations: 24.9 us -> 1.32 us
  other arithmetic: 19.9 us -> 0 us
    psum x4 -> x0, blocking collectives: 171 us -> none  [the longest x2 85.5 us: body(): lax.psum((jnp.sum(second * middle), jnp.sum(second * second), jnp.sum(sou...]
    dot_general x25 -> x0, matrix products: 155 us -> none  [the longest x5 34.4 us: to_faces(): jnp.einsum('tfc,btc->btf', local_hot, paired, precision=highest)]
    psum x5 -> x0, waiting for transfers between devices: 91.6 us -> none  [the longest x4 73.5 us: apply_matrix(): return volume_rate * vector_in + lax.psum(partial_value, 'faces')]
    gather x35 -> x0, local copies, waits for them, and re-layouts: 90.8 us -> none  [the longest x30 87.3 us: ghosts(): jnp.take(vector_in, send_list[which], axis=1)]
    pallas_call x0 -> x1, Pallas kernels: none -> 62.2 us  [body(): pl.pallas_call(functools.partial(kernel, parts, cores), out_shape=(out, o...]
    ppermute x30 -> x0, starting transfers between devices: 54.5 us -> none  [passed_along(): return lax.ppermute(block, axis, route)]
    ppermute x30 -> x0, waiting for transfers between devices: 11 us -> none  [passed_along(): return lax.ppermute(block, axis, route)]
    concatenate x4 -> x0, local copies, waits for them, and re-layouts: 10.5 us -> none  [precondition(): return jnp.concatenate([velocity, pressure[None]], axis=0)]
  transfers between devices with their start and end apart: 35 -> 0, of which waited for: 11 -> 0; matrix products, arithmetic and copies ran while one was open for 1% -> 0% of each run, Pallas kernels for 0% -> 0%
where the time goes in v1:
time: 68.2 us; the launch traced here: 68 us
  Pallas kernels  62.2 us (91%)
  local copies, waits for them, and re-layouts  4.48 us (7%)
  between operations  1.32 us (2%)
    pallas_call x1, Pallas kernels, body(): pl.pallas_call(functools.partial(kernel, parts, cores), out_shape=(out, o...  62.2 us
    unnamed x7, local copies, waits for them, and re-layouts  3.88 us

profile of v1, /device:TPU:0, one launch (start us, length us, event | category | flops | bytes accessed | tf_op | source)
XLA Modules:
  0.0 68.0 jit_solution(9691868958890863729)
XLA Ops:
  0.6 0.0 copy-start.1
  1.3 0.0 copy-done.1
  1.3 0.6 reshape.51.list_ref
  1.9 1.6 %copy.17 = f32[1,3,96,128]{3,2,1,0:T(8,128)} copy(f32[1,3,96,128]{3,1,2,0:T(4,128)} %bitcast.28) | data formatting | bytes 294912
  3.5 62.2 %shard_map.104 = (f32[256,128]{1,0:T(8,128)}, f32[256,128]{1,0:T(8,128)}) custom-call(s32[1]{0:T(128)S(6)} %copy.20.count_ref, f32[256,128]{1,0:T(8,128)} %bitcast.31, f32[256,128]{1,0:T(8,128)} %bitcast.32, f32[64,128]{1,0:T(8,128)} %bitcast.35, f32[3,96,128]{2,1,0:T(8,128)} %bitcast.27, s32[96,128]{1,0:T(8,128)} %bitcast.33, s32[96,128]{1,0:T(8,128)} %bitcast.34, ...), custom_call_target="tpu_custom_call" | custom-call | tf_op jit(solution)/shard_map/pallas_call | solution.py:486
  65.8 0.0 copy-start
  65.8 1.6 %copy.21 = f32[4,8192]{1,0:T(4,128)} copy(f32[4,8192]{1,0:T(4,128)} %bitcast.30) | data formatting | bytes 262144
  67.4 0.0 copy-done
  67.4 0.7 copy.22
Async XLA Ops:
  0.6 0.7 %copy-start.1 = (s32[6,256]{1,0:T(8,128)S(1)}, s32[6,256]{1,0:T(8,128)}, u32[]{:S(2)}) copy-start(s32[6,256]{1,0:T(8,128)} %param.16) | copy-start | bytes 18436
  65.8 1.6 %copy-start = (f32[256,128]{1,0:T(8,128)S(1)}, f32[256,128]{1,0:T(8,128)}, u32[]{:S(2)}) copy-start(f32[256,128]{1,0:T(8,128)} %get-tuple-element.5) | copy-start | bytes 393220

commit v2 on v1

--- a/solution.py
+++ b/solution.py
@@ -27,16 +27,23 @@
     parts,
     cores,
     count_ref,
+    flow_hbm,
+    source_hbm,
+    volume_hbm,
+    normal_hbm,
+    owner_hbm,
+    neighbour_hbm,
+    list_ref,
+    halo_count_ref,
+    solution_ref,
+    residual_ref,
     flow_ref,
     source_ref,
     volume_ref,
     normal_ref,
     owner_ref,
     neighbour_ref,
-    list_ref,
-    halo_count_ref,
-    solution_ref,
-    residual_ref,
+    input_sem,
     own_lane,
     right_lane,
     right_kind,
@@ -77,7 +84,21 @@
     cells = tiles * LANES
     lists = halo_in.shape[1]
     lists_here = lists // cores
-    width = list_ref.shape[2] * list_ref.shape[1]
+    width = list_ref.shape[1] * LANES
+
+    def fetched(number, source, target):
+        copy = pltpu.make_async_copy(source, target, input_sem.at[number])
+        copy.start()
+        return copy
+
+    copies = [
+        fetched(0, owner_hbm, owner_ref),
+        fetched(1, neighbour_hbm, neighbour_ref),
+        fetched(2, flow_hbm, flow_ref),
+        fetched(4, source_hbm, source_ref),
+        fetched(5, volume_hbm, volume_ref),
+    ]
+    normals = [fetched(3, normal_hbm, normal_ref)]
 
     barrier = pltpu.get_barrier_semaphore()
     for step in range(1, parts * cores):
@@ -93,6 +114,8 @@
     pair_id = lax.broadcasted_iota(jnp.int32, (pairs, LANES), 0)
     late = lane >= LANES // 2
     count = count_ref[0]
+    for copy in copies:
+        copy.wait()
     for j in range(3):
         tile = 2 * pair_id + (0 if j == 0 else 1)
         if j == 1:
@@ -110,8 +133,8 @@
         own_lane[j] = own
         right_lane[j] = jnp.where(upper, place - LANES, place)
         right_kind[j] = jnp.where(is_local, 0, 2) + upper.astype(jnp.int32)
-        own_row[j] = jnp.where(live, own, -1)
-        local_row[j] = jnp.where(live & is_local, column, -1)
+        own_row[j] = jnp.where(live, own, -1).astype(F32)
+        local_row[j] = jnp.where(live & is_local, column, -1).astype(F32)
 
     def start_halo(turn, field):
         row8 = lax.broadcasted_iota(jnp.int32, (8, LANES), 0)
@@ -164,12 +187,11 @@
         return copy
 
     def start_dots(turn, partials):
-        rows = [
-            jnp.sum(p.reshape(tiles // 8, 8, LANES).sum(axis=0), axis=0, keepdims=True)
-            for p in partials
-        ]
-        rows.append(jnp.zeros((8 - len(rows), LANES), F32))
-        packed = jnp.concatenate(rows, axis=0)
+        at = lax.broadcasted_iota(jnp.int32, (1, LANES), 1)
+        packed = jnp.zeros((1, LANES), F32)
+        for d, p in enumerate(partials):
+            row = jnp.sum(p.reshape(tiles // 8, 8, LANES).sum(axis=0), axis=0, keepdims=True)
+            packed = jnp.where(at == d, jnp.sum(row, axis=1, keepdims=True), packed)
         dot_out[turn] = packed
         dot_in[turn, me] = packed
         for step in range(1, parts):
@@ -188,8 +210,7 @@
         total = dot_in[turn, 0]
         for q in range(1, parts):
             total = total + dot_in[turn, q]
-        total = jnp.sum(total, axis=1, keepdims=True)
-        return [jnp.broadcast_to(total[d : d + 1], (1, LANES)) for d in range(number)]
+        return [jnp.broadcast_to(total[:, d : d + 1], (1, LANES)) for d in range(number)]
 
     def put_field(values, halos):
         for b, value in enumerate(values):
@@ -237,18 +258,28 @@
         ref[j, pl.ds(64 * g + b, 8, stride=8), :] = high
         ref[j, pl.ds(64 * g + 4 + b, 8, stride=8), :] = low
 
-    def scatter(rows_ref, hot_ref, cells_ref, u):
-        start = pl.multiple_of(u * 8, 8)
+    def tile_rows(rows_ref, u, odd):
+        at = pl.ds(pl.multiple_of(u * 8, 8), 8)
+        return jnp.concatenate([rows_ref[odd, at, :], rows_ref[odd + 1, at, :]], axis=1).astype(BF16)
+
+    def added(rows, hot):
+        return lax.dot_general(
+            rows, hot, (((1,), (1,)), ((), ())), preferred_element_type=F32
+        )
+
+    def scatter(u):
         for odd in range(2):
-            rows = jnp.concatenate(
-                [rows_ref[odd, pl.ds(start, 8), :], rows_ref[odd + 1, pl.ds(start, 8), :]], axis=1
-            ).astype(BF16)
-            result = lax.dot_general(
-                rows, hot_ref[2 * u + odd], (((1,), (1,)), ((), ())), preferred_element_type=F32
-            )
-            at = pl.ds(pl.multiple_of(start * 2 + odd * 8, 8), 8)
-            cells_ref[0, at, :] = result[:, :LANES]
-            cells_ref[1, at, :] = result[:, LANES:]
+            result = added(tile_rows(flux_rows, u, odd), signed_hot[2 * u + odd])
+            at = pl.ds(pl.multiple_of(u * 16 + odd * 8, 8), 8)
+            cell_rows[0, at, :] = result[:, :LANES]
+            cell_rows[1, at, :] = result[:, LANES:]
+
+    def scatter_size(u):
+        for odd in range(2):
+            rows = tile_rows(size_rows, u, odd)
+            at = pl.ds(pl.multiple_of(u * 16 + odd * 8, 8), 8)
+            size_cells[0, at, :] = added(rows, plain_hot[2 * u + odd])
+            size_cells[1, at, :] = -added(rows, signed_hot[2 * u + odd, LANES:, :])
 
     def collect(cells_ref, b):
         def rows(first, side):
@@ -276,7 +307,7 @@
                 last = n[0] * total[0] + n[1] * total[1] + n[2] * total[2] - jump[3]
                 put_flux(flux_rows, g, j, 3, last)
             for i in range(8):
-                scatter(flux_rows, signed_hot, cell_rows, g * 8 + i)
+                scatter(g * 8 + i)
             return carry
 
         lax.fori_loop(0, groups, group, 0)
@@ -317,13 +348,16 @@
     PRE, IMAGE_M, TEMP = 0, 1, 2
     flow = [flow_ref[pl.ds(b, tiles, stride=4), :] for b in range(4)]
     source = [source_ref[pl.ds(b, tiles, stride=4), :] for b in range(4)]
-    save(TEMP, flow)
     pl.semaphore_wait(barrier, parts * cores - 1)
-    start_halo(0, saved_field(TEMP))
+    start_halo(0, lambda b, g: flow_ref[pl.ds(32 * g + b, 8, stride=4), :])
     start_dots(0, [dot(source, source)])
 
-    cell_id = lax.broadcasted_iota(jnp.int32, (2 * LANES, LANES), 0)
+    cell_id = lax.broadcasted_iota(jnp.int32, (LANES, LANES), 0).astype(F32).astype(BF16)
     early_row = lax.broadcasted_iota(jnp.int32, (1, LANES), 1) < LANES // 2
+    one, zero = jnp.ones((), BF16), jnp.zeros((), BF16)
+
+    def hot_of(row):
+        return jnp.where(cell_id == row.astype(BF16), one, zero)
 
     def build(u, carry):
         for odd in range(2):
@@ -333,17 +367,19 @@
                 local = local_row[j, pl.ds(u, 1), :]
                 if j == 1:
                     keep = early_row if odd == 0 else jnp.logical_not(early_row)
-                    own = jnp.where(keep, own, -1)
-                    local = jnp.where(keep, local, -1)
-                own_hot = jnp.where(cell_id == own, 1.0, 0.0)
-                local_hot = jnp.where(cell_id == local, 1.0, 0.0)
+                    own = jnp.where(keep, own, -1.0)
+                    local = jnp.where(keep, local, -1.0)
+                own_hot, local_hot = hot_of(own), hot_of(local)
                 lanes = slice(half * LANES, (half + 1) * LANES)
-                signed_hot[2 * u + odd, :, lanes] = (own_hot - local_hot).astype(BF16)
-                plain_hot[2 * u + odd, :, lanes] = (own_hot + local_hot).astype(BF16)
+                signed_hot[2 * u + odd, :LANES, lanes] = own_hot - local_hot
+                signed_hot[2 * u + odd, LANES:, lanes] = -hot_of(local - LANES)
+                plain_hot[2 * u + odd, :, lanes] = own_hot + local_hot
         return carry
 
     lax.fori_loop(0, pairs, build, 0)
     size_rows[...] = jnp.zeros_like(size_rows)
+    for copy in normals:
+        copy.wait()
 
     put_field(flow, wait_halo(0))
 
@@ -365,8 +401,8 @@
                 put_flux(flux_rows, g, j, 1 + i, n[i])
             put_flux(size_rows, g, j, 0, s)
         for i in range(8):
-            scatter(flux_rows, signed_hot, cell_rows, g * 8 + i)
-            scatter(size_rows, plain_hot, size_cells, g * 8 + i)
+            scatter(g * 8 + i)
+            scatter_size(g * 8 + i)
         return carry
 
     lax.fori_loop(0, groups, face_terms, 0)
@@ -478,6 +514,7 @@
         return field.reshape(tiles, 4, LANES).transpose(1, 0, 2).reshape(4, cells)
 
     vmem = pl.BlockSpec(memory_space=pltpu.VMEM)
+    hbm = pl.BlockSpec(memory_space=pl.ANY)
     smem = pl.BlockSpec(memory_space=pltpu.SMEM)
     ints = pltpu.VMEM((3, pairs, LANES), jnp.int32)
     floats = pltpu.VMEM((3, pairs, LANES), F32)
@@ -486,19 +523,26 @@
     solved, left = pl.pallas_call(
         functools.partial(kernel, parts, cores),
         out_shape=(out, out),
-        in_specs=[smem] + [vmem] * 7 + [smem],
+        in_specs=[smem] + [hbm] * 6 + [vmem, smem],
         out_specs=(vmem, vmem),
         scratch_shapes=[
-            ints,
-            ints,
+            pltpu.VMEM((4 * tiles, LANES), F32),
+            pltpu.VMEM((4 * tiles, LANES), F32),
+            pltpu.VMEM((tiles, LANES), F32),
+            pltpu.VMEM((3, face_rows, LANES), F32),
+            pltpu.VMEM((face_rows, LANES), jnp.int32),
+            pltpu.VMEM((face_rows, LANES), jnp.int32),
+            pltpu.SemaphoreType.DMA((6,)),
             ints,
             ints,
             ints,
             floats,
             floats,
+            floats,
+            floats,
             pltpu.VMEM((3, 3, pairs, LANES), F32),
             hot,
-            hot,
+            pltpu.VMEM((tiles, LANES, 2 * LANES), BF16),
             pltpu.VMEM((3, 8 * pairs, LANES), F32),
             pltpu.VMEM((3, 8 * pairs, LANES), F32),
             pltpu.VMEM((2, 8 * tiles, LANES), F32),
@@ -511,8 +555,8 @@
             pltpu.VMEM((turns, 5 * tiles, LANES), F32),
             pltpu.VMEM((turns, lists // cores, 8, LANES), F32),
             pltpu.VMEM((turns, lists, 8, LANES), F32),
-            pltpu.VMEM((turns, 8, LANES), F32),
-            pltpu.VMEM((turns, parts, 8, LANES), F32),
+            pltpu.VMEM((turns + 8, 1, LANES), F32),
+            pltpu.VMEM((turns, parts + 8, 1, LANES), F32),
         ]
         + [pltpu.SemaphoreType.DMA((turns,))] * 6,
         compiler_params=pltpu.CompilerParams(

time: 68.2 us -> 66 us (0.968)
  Pallas kernels: 62.2 us -> 60 us
    pallas_call x1, Pallas kernels: 62.2 us -> 60 us  [body(): pl.pallas_call(functools.partial(kernel, parts, cores), out_shape=(out, o...]
where the time goes in v2:
time: 66 us; the launch traced here: 65.8 us
  Pallas kernels  60 us (91%)
  local copies, waits for them, and re-layouts  4.48 us (7%)
  between operations  1.32 us (2%)
    pallas_call x1, Pallas kernels, body(): pl.pallas_call(functools.partial(kernel, parts, cores), out_shape=(out, o...  60 us
    unnamed x7, local copies, waits for them, and re-layouts  3.88 us

profile of v2, /device:TPU:0, one launch (start us, length us, event | category | flops | bytes accessed | tf_op | source)
XLA Modules:
  0.0 65.8 jit_solution(13724717739032259797)
XLA Ops:
  0.6 0.0 copy-start.1
  1.3 0.0 copy-done.1
  1.3 0.6 reshape.51.list_ref
  1.9 1.6 %copy.17 = f32[1,3,96,128]{3,2,1,0:T(8,128)} copy(f32[1,3,96,128]{3,1,2,0:T(4,128)} %bitcast.28) | data formatting | bytes 294912
  3.5 60.0 %shard_map.104 = (f32[256,128]{1,0:T(8,128)}, f32[256,128]{1,0:T(8,128)}) custom-call(s32[1]{0:T(128)S(6)} %copy.20.count_ref, f32[256,128]{1,0:T(8,128)} %bitcast.31, f32[256,128]{1,0:T(8,128)} %bitcast.32, f32[64,128]{1,0:T(8,128)} %bitcast.35, f32[3,96,128]{2,1,0:T(8,128)} %bitcast.27, s32[96,128]{1,0:T(8,128)} %bitcast.33, s32[96,128]{1,0:T(8,128)} %bitcast.34, ...), custom_call_target="tpu_custom_call" | custom-call | tf_op jit(solution)/shard_map/pallas_call | solution.py:523
  63.5 0.0 copy-start
  63.5 1.6 %copy.21 = f32[4,8192]{1,0:T(4,128)} copy(f32[4,8192]{1,0:T(4,128)} %bitcast.30) | data formatting | bytes 262144
  65.1 0.0 copy-done
  65.1 0.7 copy.22
Async XLA Ops:
  0.6 0.7 %copy-start.1 = (s32[6,256]{1,0:T(8,128)S(1)}, s32[6,256]{1,0:T(8,128)}, u32[]{:S(2)}) copy-start(s32[6,256]{1,0:T(8,128)} %param.16) | copy-start | bytes 18436
  63.5 1.6 %copy-start = (f32[256,128]{1,0:T(8,128)S(1)}, f32[256,128]{1,0:T(8,128)}, u32[]{:S(2)}) copy-start(f32[256,128]{1,0:T(8,128)} %get-tuple-element.5) | copy-start | bytes 393220

commit v3 on v2

--- a/solution.py
+++ b/solution.py
@@ -98,7 +98,7 @@
         fetched(4, source_hbm, source_ref),
         fetched(5, volume_hbm, volume_ref),
     ]
-    normals = [fetched(3, normal_hbm, normal_ref)]
+    normals = [fetched(3, normal_hbm, normal_ref.at[pl.ds(0, 3 * pairs)])]
 
     barrier = pltpu.get_barrier_semaphore()
     for step in range(1, parts * cores):
@@ -386,7 +386,7 @@
     def face_terms(g, carry):
         here = pl.multiple_of(g * 8, 8)
         for j in range(3):
-            n = [normal_ref[i, pl.ds(24 * g + j, 8, stride=3), :] for i in range(3)]
+            n = [normal_ref[pl.ds(24 * g + j, 8, stride=3), i, :] for i in range(3)]
             both = [sides(g, j, b) for b in range(3)]
             total = [left + right for left, right in both]
             u = 0.5 * (n[0] * total[0] + n[1] * total[1] + n[2] * total[2])
@@ -529,7 +529,7 @@
             pltpu.VMEM((4 * tiles, LANES), F32),
             pltpu.VMEM((4 * tiles, LANES), F32),
             pltpu.VMEM((tiles, LANES), F32),
-            pltpu.VMEM((3, face_rows, LANES), F32),
+            pltpu.VMEM((face_rows + 8, 3, LANES), F32),
             pltpu.VMEM((face_rows, LANES), jnp.int32),
             pltpu.VMEM((face_rows, LANES), jnp.int32),
             pltpu.SemaphoreType.DMA((6,)),
@@ -567,7 +567,7 @@
         by_tile(flow_state),
         by_tile(source_term),
         volume_rate.reshape(tiles, LANES),
-        face_normal.reshape(3, face_rows, LANES),
+        face_normal.reshape(3, face_rows, LANES).transpose(1, 0, 2),
         face_owner.reshape(face_rows, LANES),
         face_neighbour.reshape(face_rows, LANES),
         send_list.reshape(lists, width // LANES, LANES),

time: 66 us -> 64.7 us (0.980)
  local copies, waits for them, and re-layouts: 4.48 us -> 2.9 us
    unnamed x7 -> x6, local copies, waits for them, and re-layouts: 3.88 us -> 2.29 us
where the time goes in v3:
time: 64.7 us; the launch traced here: 64.4 us
  Pallas kernels  60.2 us (93%)
  local copies, waits for them, and re-layouts  2.9 us (4%)
  between operations  1.31 us (2%)
    pallas_call x1, Pallas kernels, body(): pl.pallas_call(functools.partial(kernel, parts, cores), out_shape=(out, o...  60.2 us
    unnamed x6, local copies, waits for them, and re-layouts  2.29 us

profile of v3, /device:TPU:0, one launch (start us, length us, event | category | flops | bytes accessed | tf_op | source)
XLA Modules:
  0.0 64.4 jit_solution(3804672061715814383)
XLA Ops:
  0.6 0.0 copy-start.1
  1.3 0.0 copy-done.1
  1.3 0.6 reshape.51.list_ref
  1.9 60.2 %shard_map.104 = (f32[256,128]{1,0:T(8,128)}, f32[256,128]{1,0:T(8,128)}) custom-call(s32[1]{0:T(128)S(6)} %copy.17.count_ref, f32[256,128]{1,0:T(8,128)} %bitcast.29, f32[256,128]{1,0:T(8,128)} %bitcast.30, f32[64,128]{1,0:T(8,128)} %bitcast.33, f32[96,3,128]{2,1,0:T(4,128)} %bitcast.26, s32[96,128]{1,0:T(8,128)} %bitcast.31, s32[96,128]{1,0:T(8,128)} %bitcast.32, ...), custom_call_target="tpu_custom_call" | custom-call | tf_op jit(solution)/shard_map/pallas_call | solution.py:523
  62.1 0.0 copy-start
  62.2 1.6 %copy.18 = f32[4,8192]{1,0:T(4,128)} copy(f32[4,8192]{1,0:T(4,128)} %bitcast.28) | data formatting | bytes 262144
  63.8 0.0 copy-done
  63.8 0.7 %copy.19 = f32[4,8192]{1,0:T(4,128)} copy(f32[4,8192]{1,0:T(4,128)S(1)} %bitcast.27) | data formatting | bytes 262144
Async XLA Ops:
  0.6 0.7 %copy-start.1 = (s32[6,256]{1,0:T(8,128)S(1)}, s32[6,256]{1,0:T(8,128)}, u32[]{:S(2)}) copy-start(s32[6,256]{1,0:T(8,128)} %param.16) | copy-start | bytes 18436
  62.1 1.6 %copy-start = (f32[256,128]{1,0:T(8,128)S(1)}, f32[256,128]{1,0:T(8,128)}, u32[]{:S(2)}) copy-start(f32[256,128]{1,0:T(8,128)} %get-tuple-element.5) | copy-start | bytes 393220
